TPU v7x, 256 devices: a whole 4x4x8 slice. The times are simulated.
256 devices in a mesh: row: 8 (over z), col: 16 (over y_lo, x, core), layer: 2 (over y_hi).
Axes of the slice: x: 4, y: 4 (y_hi: 2, y_lo: 2; y = y_hi * 2 + y_lo), z: 8, core: 2. Of those that a mesh axis runs over, the one named last changes fastest.
Arguments:
- left: bfloat16 [8192, 8192], P('row', ('col', 'layer')), may hold values from -6 to 6
- middle: bfloat16 [8192, 8192], P('row', 'col'), may hold values from -0.0625 to 0.0625
- right: bfloat16 [8192, 8192], P('row', 'col'), may hold values from -0.0625 to 0.0625
Outputs:
- product: bfloat16 [8192, 8192], P('row', ('col', 'layer'))
All inputs are finite; a program needn't handle non-finite values.
Results may differ from a plain program's by a relative error of at most 0.0049.
Values may be sent and summed in bfloat16 or wider, within the bound.
A program may use at most 64 MiB of HBM per device.

v0:
```python
import jax
import jax.numpy as jnp
from jax import lax
from jax.sharding import PartitionSpec as P


def split_up(array, dim, size):
    lengths = array.shape
    blocks = array.reshape(*lengths[:dim], size, lengths[dim] // size, *lengths[dim + 1 :])
    return jnp.moveaxis(blocks, dim, 0)


def sum_at_owner(array, axis, dim):
    blocks = split_up(array, dim, lax.axis_size(axis))
    arrived = lax.all_to_all(blocks, axis, split_axis=0, concat_axis=0, tiled=True)
    return arrived.sum(axis=0)


def multiply(left, right):
    width = left.shape[1]
    layers = lax.axis_size("layer")
    layer_index = lax.axis_index("layer")
    columns = right.shape[1]
    groups = right.shape[0] // width // layers
    shaped = right.reshape(groups, layers, width, columns)
    own_rows = lax.dynamic_index_in_dim(shaped, layer_index, 1, keepdims=False).reshape(
        groups * width, columns
    )
    right_all = lax.all_gather(own_rows, "row", axis=0, tiled=True)
    return jnp.dot(
        lax.all_gather(left, "col", axis=1, tiled=True),
        right_all,
        preferred_element_type=jnp.float32,
    )


def per_device(left, middle, right):
    partial_value = multiply(left, middle)
    first = sum_at_owner(partial_value, "layer", 1)
    first = first.astype(jnp.bfloat16)
    second = multiply(first, right)
    return sum_at_owner(second, "layer", 1).astype(jnp.bfloat16)


def solution(mesh):
    return jax.shard_map(
        per_device,
        mesh=mesh,
        in_specs=(P("row", ("col", "layer")), P("row", "col"), P("row", "col")),
        out_specs=P("row", ("col", "layer")),
        check_vma=False,
    )
```

profile of v0, /device:TPU:1, one launch (start us, length us, event | category | flops | bytes accessed | tf_op | source)
XLA Modules:
  0.0 290.7 jit_solution(16866077000397679622)
XLA Ops:
  6.5 0.0 copy-start
  6.5 0.0 all-gather.5.cloned.1.call-start
  6.5 1.2 copy-done
  7.8 0.8 constant_dynamic-slice_fusion.1
  8.6 0.0 all-gather.5.cloned.1.call-update
  8.6 0.0 all-gather.7.cloned.1.call-start
  8.7 0.7 all-gather.7.cloned.1.call-update
  9.4 0.0 all-gather.11.cloned.1.call-start
  9.4 1.9 constant_dynamic-slice_fusion
  11.3 0.0 all-gather.11.cloned.1.call-update
  11.3 0.0 all-gather.9.cloned.1.call-start
  11.4 56.2 %all-gather.5.cloned.1.call-done = bf16[4096,512]{1,0:T(8,128)(2,1)} async-done(((bf16[512,512]{1,0:T(8,128)(2,1)}), bf16[4096,512]{1,0:T(8,128)(2,1)}) %all-gather.5.cloned.1.call-update) | async-done | bytes 4194320 | tf_op jit(solution)/shard_map/all_gather | solution.py:29
  67.5 64.4 %all-gather.7.cloned.1.call-done = bf16[1024,4096]{1,0:T(8,128)(2,1)} async-done(((bf16[1024,256]{1,0:T(8,128)(2,1)}), bf16[1024,4096]{1,0:T(8,128)(2,1)}) %all-gather.7.cloned.1.call-update) | async-done | bytes 8388624 | tf_op jit(solution)/shard_map/all_gather | solution.py:31
  131.9 8.2 %fusion = f32[512,1024]{1,0:T(8,128)S(1)} fusion(bf16[4096,512]{1,0:T(8,128)(2,1)} %all-gather.5.cloned.1.call-done, bf16[1024,4096]{1,0:T(8,128)(2,1)} %all-gather.7.cloned.1.call-done), kind=kOutput, calls=%fused_computation.2 | convolution fusion | flops 4294967296 | bytes 14680064 | tf_op jit(solution)/shard_map/dot_general | solution.py:30
  140.1 28.8 %all_to_all.10 = f32[2,1024,256]{1,2,0:T(8,128)S(1)} all-to-all(f32[2,1024,256]{1,2,0:T(8,128)S(1)} %bitcast.17), channel_id=1, replica_groups=mesh['row'=8,'col'=16,'layer'=2] {'layer'}, dimensions={0} | all-to-all | bytes 4194304 | tf_op jit(solution)/shard_map/all_to_all | solution.py:15
  168.9 1.1 reduce_sum.18
  170.0 0.0 all-gather.9.cloned.1.call-update
  170.0 17.7 %all-gather.11.cloned.1.call-done = bf16[4096,512]{1,0:T(8,128)(2,1)} async-done(((bf16[512,512]{1,0:T(8,128)(2,1)}), bf16[4096,512]{1,0:T(8,128)(2,1)}) %all-gather.11.cloned.1.call-update) | async-done | bytes 4194320 | tf_op jit(solution)/shard_map/all_gather | solution.py:29
  187.7 55.5 %all-gather.9.cloned.1.call-done = bf16[1024,4096]{0,1:T(8,128)(2,1)} async-done(((bf16[1024,256]{0,1:T(8,128)(2,1)}), bf16[1024,4096]{0,1:T(8,128)(2,1)}) %all-gather.9.cloned.1.call-update) | async-done | bytes 8388624 | tf_op jit(solution)/shard_map/all_gather | solution.py:31
  243.2 8.2 %fusion.1 = f32[1024,512]{0,1:T(8,128)S(1)} fusion(bf16[1024,4096]{0,1:T(8,128)(2,1)} %all-gather.9.cloned.1.call-done, bf16[4096,512]{1,0:T(8,128)(2,1)} %all-gather.11.cloned.1.call-done), kind=kOutput, calls=%fused_computation.3 | convolution fusion | flops 4294967296 | bytes 14680064 | tf_op jit(solution)/shard_map/dot_general | solution.py:30
  251.4 29.6 %all_to_all.11 = f32[2,1024,256]{1,2,0:T(8,128)S(1)} all-to-all(f32[2,1024,256]{1,2,0:T(8,128)S(1)} %bitcast.18), channel_id=1, replica_groups=mesh['row'=8,'col'=16,'layer'=2] {'layer'}, dimensions={0} | all-to-all | bytes 4194304 | tf_op jit(solution)/shard_map/all_to_all | solution.py:15
  281.0 1.1 reduce_sum.19
  282.1 2.0 copy.4
Async XLA Ops:
  6.5 1.2 copy-start
  6.5 61.0 %all-gather.5.cloned.1.call-start = ((), (), s32[]{:S(2)}) async-start(), calls=%async_computation.2 | async-start | bytes 4718592 | tf_op jit(solution)/shard_map/all_gather | solution.py:29
  8.6 123.3 %all-gather.7.cloned.1.call-start = ((), (), s32[]{:S(2)}) async-start(), calls=%async_computation.3 | async-start | bytes 8912896 | tf_op jit(solution)/shard_map/all_gather | solution.py:31
  9.4 178.3 %all-gather.11.cloned.1.call-start = ((), (), s32[]{:S(2)}) async-start(), calls=%async_computation.5 | async-start | bytes 4718592 | tf_op jit(solution)/shard_map/all_gather | solution.py:29
  11.3 231.9 %all-gather.9.cloned.1.call-start = ((), (), s32[]{:S(2)}) async-start(), calls=%async_computation.4 | async-start | bytes 8912896 | tf_op jit(solution)/shard_map/all_gather | solution.py:31
Sparse Core Ops, SparseCore 0:
  9.1 58.3 all-gather.4
  69.3 62.5 all-gather.6
  133.7 53.9 all-gather.10
  189.4 53.7 all-gather.8
where the time goes:
time: 291 us
  waiting for transfers between devices  194 us (67%)
  blocking collectives  58.3 us (20%)
  matrix products  16.5 us (6%)
  between operations  13.1 us (5%)
  local copies, waits for them, and re-layouts  5.97 us (2%)
    all_gather x2, waiting for transfers between devices, multiply(): lax.all_gather(left, 'col', axis=1, tiled=True)  120 us
    all_gather x2, waiting for transfers between devices, multiply(): right_all = lax.all_gather(own_rows, 'row', axis=0, tiled=True)  73.8 us
    all_to_all x2, blocking collectives, sum_at_owner(): lax.all_to_all(blocks, axis, split_axis=0, concat_axis=0, tiled=True)  58.3 us
    dot_general x2, matrix products, multiply(): jnp.dot(lax.all_gather(left, 'col', axis=1, tiled=True), right_all, prefe...  16.5 us
  transfers between devices with their start and end apart: 4, of which 4 were waited for; matrix products, arithmetic and copies ran while one was open for 4% of the time, Pallas kernels for 0%

commit v1 on v0

--- a/solution.py
+++ b/solution.py
@@ -2,6 +2,25 @@
 import jax.numpy as jnp
 from jax import lax
 from jax.sharding import PartitionSpec as P
+
+
+def launch_axis_part(raw, out_dim):
+    front = list(raw.shape[1:])
+    front[out_dim] *= raw.shape[0]
+    part_now = jnp.moveaxis(raw, 0, out_dim).reshape(front)
+    return part_now
+
+
+def entries_rest(values, axis_name, dim_no):
+    world = lax.axis_size(axis_name)
+    grid = [(at, (at + 1) % world) for at in range(world)]
+    leaves = [values]
+    while len(leaves) < world:
+        leaves.append(lax.ppermute(leaves[-1], axis_name, grid))
+    o_now = lax.axis_index(axis_name)
+    leaves = jnp.stack(leaves)[(o_now - jnp.arange(world)) % world]
+    out_arr = launch_axis_part(leaves, dim_no)
+    return out_arr
 
 
 def split_up(array, dim, size):
@@ -26,7 +45,7 @@
     own_rows = lax.dynamic_index_in_dim(shaped, layer_index, 1, keepdims=False).reshape(
         groups * width, columns
     )
-    right_all = lax.all_gather(own_rows, "row", axis=0, tiled=True)
+    right_all = entries_rest(own_rows, "row", 0)
     return jnp.dot(
         lax.all_gather(left, "col", axis=1, tiled=True),
         right_all,

time: 291 us -> 288 us (0.990)
  the two profiles are of different devices: /device:TPU:1 before, /device:TPU:4 now
where the time goes in v1:
time: 288 us; the launch traced here: 287 us
  waiting for transfers between devices  174 us (60%)
  blocking collectives  43.7 us (15%)
  local copies, waits for them, and re-layouts  35.6 us (12%)
  matrix products  16.4 us (6%)
  between operations  13.5 us (5%)
    ppermute x14, waiting for transfers between devices, entries_rest(): leaves.append(lax.ppermute(leaves[-1], axis_name, grid))  173 us
    all_to_all x2, blocking collectives, sum_at_owner(): lax.all_to_all(blocks, axis, split_axis=0, concat_axis=0, tiled=True)  43.7 us
    dot_general x2, matrix products, multiply(): jnp.dot(lax.all_gather(left, 'col', axis=1, tiled=True), right_all, prefe...  16.4 us
    unnamed x18, local copies, waits for them, and re-layouts  14.4 us
    gather x2, local copies, waits for them, and re-layouts, entries_rest(): leaves = jnp.stack(leaves)[(o_now - jnp.arange(world)) % world]  9.91 us
    dot_general x1, local copies, waits for them, and re-layouts, multiply(): jnp.dot(lax.all_gather(left, 'col', axis=1, tiled=True), right_all, prefe...  6.44 us
  transfers between devices with their start and end apart: 16, of which 14 were waited for; matrix products, arithmetic and copies ran while one was open for 12% of the time, Pallas kernels for 0%

profile of v1, /device:TPU:4, one launch (start us, length us, event | category | flops | bytes accessed | tf_op | source)
XLA Modules:
  0.0 287.0 jit_solution(18411777771239815482)
XLA Ops:
  7.8 2.0 collective-permute-start
  9.8 15.9 %collective-permute-done = bf16[512,512]{1,0:T(8,128)(2,1)S(1)} collective-permute-done((bf16[512,512]{1,0:T(8,128)(2,1)S(1)}, bf16[512,512]{1,0:T(8,128)(2,1)S(1)}, u32[]{:S(2)}, u32[]{:S(2)}) %collective-permute-start) | collective-permute-done | bytes 524320 | tf_op jit(solution)/shard_map/ppermute | solution.py:19
  25.7 14.3 %collective-permute-done.1 = bf16[512,512]{1,0:T(8,128)(2,1)S(1)} collective-permute-done((bf16[512,512]{1,0:T(8,128)(2,1)S(1)}, bf16[512,512]{1,0:T(8,128)(2,1)S(1)}, u32[]{:S(2)}, u32[]{:S(2)}) %collective-permute-start.1) | collective-permute-done | bytes 524320 | tf_op jit(solution)/shard_map/ppermute | solution.py:19
  40.0 13.4 %collective-permute-done.2 = bf16[512,512]{1,0:T(8,128)(2,1)S(1)} collective-permute-done((bf16[512,512]{1,0:T(8,128)(2,1)S(1)}, bf16[512,512]{1,0:T(8,128)(2,1)S(1)}, u32[]{:S(2)}, u32[]{:S(2)}) %collective-permute-start.2) | collective-permute-done | bytes 524320 | tf_op jit(solution)/shard_map/ppermute | solution.py:19
  53.4 12.6 %collective-permute-done.3 = bf16[512,512]{1,0:T(8,128)(2,1)S(1)} collective-permute-done((bf16[512,512]{1,0:T(8,128)(2,1)S(1)}, bf16[512,512]{1,0:T(8,128)(2,1)S(1)}, u32[]{:S(2)}, u32[]{:S(2)}) %collective-permute-start.3) | collective-permute-done | bytes 524320 | tf_op jit(solution)/shard_map/ppermute | solution.py:19
  66.9 11.0 %collective-permute-done.4 = bf16[512,512]{1,0:T(8,128)(2,1)} collective-permute-done((bf16[512,512]{1,0:T(8,128)(2,1)S(1)}, bf16[512,512]{1,0:T(8,128)(2,1)}, u32[]{:S(2)}, u32[]{:S(2)}) %collective-permute-start.4) | collective-permute-done | bytes 524320 | tf_op jit(solution)/shard_map/ppermute | solution.py:19
  81.4 8.8 %collective-permute-done.5 = bf16[512,512]{1,0:T(8,128)(2,1)S(1)} collective-permute-done((bf16[512,512]{1,0:T(8,128)(2,1)}, bf16[512,512]{1,0:T(8,128)(2,1)S(1)}, u32[]{:S(2)}, u32[]{:S(2)}) %collective-permute-start.5) | collective-permute-done | bytes 524320 | tf_op jit(solution)/shard_map/ppermute | solution.py:19
  91.0 1.9 bitcast_dynamic-update-slice_fusion.9
  93.7 6.8 %collective-permute-done.6 = bf16[512,512]{1,0:T(8,128)(2,1)S(1)} collective-permute-done((bf16[512,512]{1,0:T(8,128)(2,1)S(1)}, bf16[512,512]{1,0:T(8,128)(2,1)S(1)}, u32[]{:S(2)}, u32[]{:S(2)}) %collective-permute-start.6) | collective-permute-done | bytes 524320 | tf_op jit(solution)/shard_map/ppermute | solution.py:19
  101.4 5.0 %gather_fusion = bf16[8,512,512]{2,1,0:T(8,128)(2,1)} fusion(bf16[8,512,512]{2,1,0:T(8,128)(2,1)} %bitcast_dynamic-update-slice_fusion.7, s32[1024]{0:T(1024)S(1)} %pad_clamp_fusion), kind=kCustom, calls=%fused_computation | custom fusion | bytes 8388640 | tf_op jit(solution)/shard_map/gather | solution.py:21
  106.4 8.2 %fusion.7 = f32[512,1024]{1,0:T(8,128)S(1)} fusion(bf16[4096,512]{1,0:T(8,128)(2,1)} %bitcast.62, bf16[1024,4096]{1,0:T(8,128)(2,1)} %all-gather.3.cloned.1.call-done), kind=kOutput, calls=%fused_computation.30 | convolution fusion | flops 4294967296 | bytes 14680064 | tf_op jit(solution)/shard_map/dot_general | solution.py:49
  114.6 24.6 %all_to_all.10 = f32[2,1024,256]{1,2,0:T(8,128)S(1)} all-to-all(f32[2,1024,256]{1,2,0:T(8,128)S(1)} %bitcast.63), channel_id=1, replica_groups=mesh['row'=8,'col'=16,'layer'=2] {'layer'}, dimensions={0} | all-to-all | bytes 4194304 | tf_op jit(solution)/shard_map/all_to_all | solution.py:34
  140.3 2.0 copy.6
  143.6 15.0 %collective-permute-done.7 = bf16[512,512]{1,0:T(8,128)(2,1)S(1)} collective-permute-done((bf16[512,512]{1,0:T(8,128)(2,1)S(1)}, bf16[512,512]{1,0:T(8,128)(2,1)S(1)}, u32[]{:S(2)}, u32[]{:S(2)}) %collective-permute-start.7) | collective-permute-done | bytes 524320 | tf_op jit(solution)/shard_map/ppermute | solution.py:19
  158.6 15.8 %collective-permute-done.8 = bf16[512,512]{1,0:T(8,128)(2,1)S(1)} collective-permute-done((bf16[512,512]{1,0:T(8,128)(2,1)S(1)}, bf16[512,512]{1,0:T(8,128)(2,1)S(1)}, u32[]{:S(2)}, u32[]{:S(2)}) %collective-permute-start.8) | collective-permute-done | bytes 524320 | tf_op jit(solution)/shard_map/ppermute | solution.py:19
  174.4 15.0 %collective-permute-done.9 = bf16[512,512]{1,0:T(8,128)(2,1)S(1)} collective-permute-done((bf16[512,512]{1,0:T(8,128)(2,1)S(1)}, bf16[512,512]{1,0:T(8,128)(2,1)S(1)}, u32[]{:S(2)}, u32[]{:S(2)}) %collective-permute-start.9) | collective-permute-done | bytes 524320 | tf_op jit(solution)/shard_map/ppermute | solution.py:19
  189.4 14.1 %collective-permute-done.10 = bf16[512,512]{1,0:T(8,128)(2,1)S(1)} collective-permute-done((bf16[512,512]{1,0:T(8,128)(2,1)S(1)}, bf16[512,512]{1,0:T(8,128)(2,1)S(1)}, u32[]{:S(2)}, u32[]{:S(2)}) %collective-permute-start.10) | collective-permute-done | bytes 524320 | tf_op jit(solution)/shard_map/ppermute | solution.py:19
  204.4 12.4 %collective-permute-done.11 = bf16[512,512]{1,0:T(8,128)(2,1)S(1)} collective-permute-done((bf16[512,512]{1,0:T(8,128)(2,1)S(1)}, bf16[512,512]{1,0:T(8,128)(2,1)S(1)}, u32[]{:S(2)}, u32[]{:S(2)}) %collective-permute-start.11) | collective-permute-done | bytes 524320 | tf_op jit(solution)/shard_map/ppermute | solution.py:19
  219.4 9.8 %collective-permute-done.12 = bf16[512,512]{1,0:T(8,128)(2,1)S(1)} collective-permute-done((bf16[512,512]{1,0:T(8,128)(2,1)S(1)}, bf16[512,512]{1,0:T(8,128)(2,1)S(1)}, u32[]{:S(2)}, u32[]{:S(2)}) %collective-permute-start.12) | collective-permute-done | bytes 524320 | tf_op jit(solution)/shard_map/ppermute | solution.py:19
  231.7 7.9 %collective-permute-done.13 = bf16[512,512]{1,0:T(8,128)(2,1)S(1)} collective-permute-done((bf16[512,512]{1,0:T(8,128)(2,1)S(1)}, bf16[512,512]{1,0:T(8,128)(2,1)S(1)}, u32[]{:S(2)}, u32[]{:S(2)}) %collective-permute-start.13) | collective-permute-done | bytes 524320 | tf_op jit(solution)/shard_map/ppermute | solution.py:19
  240.4 4.9 %gather_fusion.1 = bf16[8,512,512]{2,1,0:T(8,128)(2,1)} fusion(bf16[8,512,512]{2,1,0:T(8,128)(2,1)} %bitcast_dynamic-update-slice_fusion, s32[1024]{0:T(1024)S(1)} %pad_clamp_fusion), kind=kCustom, calls=%fused_computation.1 | custom fusion | bytes 8388640 | tf_op jit(solution)/shard_map/gather | solution.py:21
  245.4 6.4 %copy.8 = bf16[512,4096]{1,0:T(8,128)(2,1)} copy(bf16[512,4096]{0,1:T(8,128)(2,1)} %bitcast.60) | data formatting | bytes 8388608 | tf_op jit(solution)/shard_map/dot_general | solution.py:49
  251.8 8.2 %fusion.2 = f32[2,1024,256]{2,1,0:T(8,128)S(1)} fusion(bf16[2,256,4096]{2,1,0:T(8,128)(2,1)} %bitcast.61, bf16[1024,4096]{1,0:T(8,128)(2,1)} %all-gather.5.cloned.1.call-done), kind=kOutput, calls=%fused_computation.4 | convolution fusion | flops 4294967296 | bytes 14680064 | tf_op jit(solution)/shard_map/dot_general | solution.py:49
  260.0 19.1 %all_to_all.11 = f32[2,1024,256]{2,1,0:T(8,128)S(1)} all-to-all(f32[2,1024,256]{2,1,0:T(8,128)S(1)} %fusion.2), channel_id=1, replica_groups=mesh['row'=8,'col'=16,'layer'=2] {'layer'}, dimensions={0} | all-to-all | bytes 4194304 | tf_op jit(solution)/shard_map/all_to_all | solution.py:34
  (44 shorter events, 18.4 us)
Async XLA Ops:
  6.5 1.2 copy-start
  6.5 99.9 %all-gather.3.cloned.1.call-start = ((), (), s32[]{:S(2)}) async-start(), calls=%async_computation.2 | async-start | bytes 8912896 | tf_op jit(solution)/shard_map/all_gather | solution.py:50
  7.3 244.6 %all-gather.5.cloned.1.call-start = ((), (), s32[]{:S(2)}) async-start(), calls=%async_computation.3 | async-start | bytes 8912896 | tf_op jit(solution)/shard_map/all_gather | solution.py:50
  7.8 17.9 %collective-permute-start = (bf16[512,512]{1,0:T(8,128)(2,1)S(1)}, bf16[512,512]{1,0:T(8,128)(2,1)S(1)}, u32[]{:S(2)}, u32[]{:S(2)}) collective-permute-start(bf16[512,512]{1,0:T(8,128)(2,1)S(1)} %bitcast.64), channel_id=1, source_target_pairs={{0,32},{32,64},{64,96},{96,128},{128,160},{160,192},{192,224},{224... | collective-permute-start | bytes 1572872 | tf_op jit(solution)/shard_map/ppermute | solution.py:19
  25.7 14.3 %collective-permute-start.1 = (bf16[512,512]{1,0:T(8,128)(2,1)S(1)}, bf16[512,512]{1,0:T(8,128)(2,1)S(1)}, u32[]{:S(2)}, u32[]{:S(2)}) collective-permute-start(bf16[512,512]{1,0:T(8,128)(2,1)S(1)} %collective-permute-done), channel_id=1, source_target_pairs={{0,32},{32,64},{64,96},{96,128},{128,160},{160,192},{192,224},{224... | collective-permute-start | bytes 1572872 | tf_op jit(solution)/shard_map/ppermute | solution.py:19
  40.0 13.4 %collective-permute-start.2 = (bf16[512,512]{1,0:T(8,128)(2,1)S(1)}, bf16[512,512]{1,0:T(8,128)(2,1)S(1)}, u32[]{:S(2)}, u32[]{:S(2)}) collective-permute-start(bf16[512,512]{1,0:T(8,128)(2,1)S(1)} %collective-permute-done.1), channel_id=1, source_target_pairs={{0,32},{32,64},{64,96},{96,128},{128,160},{160,192},{192,224},{224... | collective-permute-start | bytes 1572872 | tf_op jit(solution)/shard_map/ppermute | solution.py:19
  53.4 12.6 %copy-start.1 = (bf16[512,512]{1,0:T(8,128)(2,1)}, bf16[512,512]{1,0:T(8,128)(2,1)S(1)}, u32[]{:S(2)}) copy-start(bf16[512,512]{1,0:T(8,128)(2,1)S(1)} %collective-permute-done.2) | copy-start | bytes 1572868
  53.4 12.6 %collective-permute-start.3 = (bf16[512,512]{1,0:T(8,128)(2,1)S(1)}, bf16[512,512]{1,0:T(8,128)(2,1)S(1)}, u32[]{:S(2)}, u32[]{:S(2)}) collective-permute-start(bf16[512,512]{1,0:T(8,128)(2,1)S(1)} %collective-permute-done.2), channel_id=1, source_target_pairs={{0,32},{32,64},{64,96},{96,128},{128,160},{160,192},{192,224},{224... | collective-permute-start | bytes 1572872 | tf_op jit(solution)/shard_map/ppermute | solution.py:19
  66.0 11.9 %collective-permute-start.4 = (bf16[512,512]{1,0:T(8,128)(2,1)S(1)}, bf16[512,512]{1,0:T(8,128)(2,1)}, u32[]{:S(2)}, u32[]{:S(2)}) collective-permute-start(bf16[512,512]{1,0:T(8,128)(2,1)S(1)} %collective-permute-done.3), channel_id=1, source_target_pairs={{0,32},{32,64},{64,96},{96,128},{128,160},{160,192},{192,224},{224... | collective-permute-start | bytes 1572872 | tf_op jit(solution)/shard_map/ppermute | solution.py:19
  77.9 12.3 %collective-permute-start.5 = (bf16[512,512]{1,0:T(8,128)(2,1)}, bf16[512,512]{1,0:T(8,128)(2,1)S(1)}, u32[]{:S(2)}, u32[]{:S(2)}) collective-permute-start(bf16[512,512]{1,0:T(8,128)(2,1)} %collective-permute-done.4), channel_id=1, source_target_pairs={{0,32},{32,64},{64,96},{96,128},{128,160},{160,192},{192,224},{224... | collective-permute-start | bytes 1572872 | tf_op jit(solution)/shard_map/ppermute | solution.py:19
  90.2 10.4 %collective-permute-start.6 = (bf16[512,512]{1,0:T(8,128)(2,1)S(1)}, bf16[512,512]{1,0:T(8,128)(2,1)S(1)}, u32[]{:S(2)}, u32[]{:S(2)}) collective-permute-start(bf16[512,512]{1,0:T(8,128)(2,1)S(1)} %collective-permute-done.5), channel_id=1, source_target_pairs={{0,32},{32,64},{64,96},{96,128},{128,160},{160,192},{192,224},{224... | collective-permute-start | bytes 1572872 | tf_op jit(solution)/shard_map/ppermute | solution.py:19
  143.5 15.1 %collective-permute-start.7 = (bf16[512,512]{1,0:T(8,128)(2,1)S(1)}, bf16[512,512]{1,0:T(8,128)(2,1)S(1)}, u32[]{:S(2)}, u32[]{:S(2)}) collective-permute-start(bf16[512,512]{1,0:T(8,128)(2,1)S(1)} %bitcast.66), channel_id=1, source_target_pairs={{0,32},{32,64},{64,96},{96,128},{128,160},{160,192},{192,224},{224... | collective-permute-start | bytes 1572872 | tf_op jit(solution)/shard_map/ppermute | solution.py:19
  158.6 15.8 %collective-permute-start.8 = (bf16[512,512]{1,0:T(8,128)(2,1)S(1)}, bf16[512,512]{1,0:T(8,128)(2,1)S(1)}, u32[]{:S(2)}, u32[]{:S(2)}) collective-permute-start(bf16[512,512]{1,0:T(8,128)(2,1)S(1)} %collective-permute-done.7), channel_id=1, source_target_pairs={{0,32},{32,64},{64,96},{96,128},{128,160},{160,192},{192,224},{224... | collective-permute-start | bytes 1572872 | tf_op jit(solution)/shard_map/ppermute | solution.py:19
  174.4 15.0 %collective-permute-start.9 = (bf16[512,512]{1,0:T(8,128)(2,1)S(1)}, bf16[512,512]{1,0:T(8,128)(2,1)S(1)}, u32[]{:S(2)}, u32[]{:S(2)}) collective-permute-start(bf16[512,512]{1,0:T(8,128)(2,1)S(1)} %collective-permute-done.8), channel_id=1, source_target_pairs={{0,32},{32,64},{64,96},{96,128},{128,160},{160,192},{192,224},{224... | collective-permute-start | bytes 1572872 | tf_op jit(solution)/shard_map/ppermute | solution.py:19
  189.4 14.1 %collective-permute-start.10 = (bf16[512,512]{1,0:T(8,128)(2,1)S(1)}, bf16[512,512]{1,0:T(8,128)(2,1)S(1)}, u32[]{:S(2)}, u32[]{:S(2)}) collective-permute-start(bf16[512,512]{1,0:T(8,128)(2,1)S(1)} %collective-permute-done.9), channel_id=1, source_target_pairs={{0,32},{32,64},{64,96},{96,128},{128,160},{160,192},{192,224},{224... | collective-permute-start | bytes 1572872 | tf_op jit(solution)/shard_map/ppermute | solution.py:19
  203.5 13.3 %collective-permute-start.11 = (bf16[512,512]{1,0:T(8,128)(2,1)S(1)}, bf16[512,512]{1,0:T(8,128)(2,1)S(1)}, u32[]{:S(2)}, u32[]{:S(2)}) collective-permute-start(bf16[512,512]{1,0:T(8,128)(2,1)S(1)} %collective-permute-done.10), channel_id=1, source_target_pairs={{0,32},{32,64},{64,96},{96,128},{128,160},{160,192},{192,224},{224... | collective-permute-start | bytes 1572872 | tf_op jit(solution)/shard_map/ppermute | solution.py:19
  216.8 12.4 %collective-permute-start.12 = (bf16[512,512]{1,0:T(8,128)(2,1)S(1)}, bf16[512,512]{1,0:T(8,128)(2,1)S(1)}, u32[]{:S(2)}, u32[]{:S(2)}) collective-permute-start(bf16[512,512]{1,0:T(8,128)(2,1)S(1)} %collective-permute-done.11), channel_id=1, source_target_pairs={{0,32},{32,64},{64,96},{96,128},{128,160},{160,192},{192,224},{224... | collective-permute-start | bytes 1572872 | tf_op jit(solution)/shard_map/ppermute | solution.py:19
  229.2 10.4 %collective-permute-start.13 = (bf16[512,512]{1,0:T(8,128)(2,1)S(1)}, bf16[512,512]{1,0:T(8,128)(2,1)S(1)}, u32[]{:S(2)}, u32[]{:S(2)}) collective-permute-start(bf16[512,512]{1,0:T(8,128)(2,1)S(1)} %collective-permute-done.12), channel_id=1, source_target_pairs={{0,32},{32,64},{64,96},{96,128},{128,160},{160,192},{192,224},{224... | collective-permute-start | bytes 1572872 | tf_op jit(solution)/shard_map/ppermute | solution.py:19
Sparse Core Ops, SparseCore 0:
  9.1 65.5 all-gather.2
  142.5 58.5 all-gather.4
